TPU v7x, 32 devices: a whole 2x2x4 slice. The times are simulated.
32 devices in a mesh: gx: 2 (over core), gy: 4 (over y, x), gz: 4 (over z).
Axes of the slice: x: 2, y: 2, z: 4, core: 2. Of those that a mesh axis runs over, the one named last changes fastest.
Arguments:
- velocity: float32 [3, 16, 64, 512], P(None, 'gx', 'gy', 'gz'), may hold values from -6 to 6
- diffusion: float32 [3], replicated, may hold values from 0.5 to 4
Outputs:
- viscous_velocity: float32 [3, 16, 64, 512], P(None, 'gx', 'gy', 'gz')
- residual: float32 [3, 16, 64, 512], P(None, 'gx', 'gy', 'gz')
All inputs are finite; a program needn't handle non-finite values.
Results may differ from a plain program's by a relative error of at most 0.0003.
Values sent between devices are 32-bit elements; how exact they have to be, the bound alone decides.
A program may use at most 64 MiB of HBM per device.

v0:
```python
import jax
import jax.numpy as jnp
from jax import lax
from jax.sharding import PartitionSpec as P

ITERS = 3


time_step = 0.25


def with_halo(value, sides, width):
    for axis, dim in sides:
        size, length = (lax.axis_size(axis), value.shape[dim])
        up = [(i, (i + 1) % size) for i in range(size - 1)]
        down = [(j, i) for i, j in up]
        last = lax.slice_in_dim(value, length - width, length, axis=dim)
        first = lax.slice_in_dim(value, 0, width, axis=dim)
        before = lax.ppermute(last, axis, up)
        after = lax.ppermute(first, axis, down)
        value = jnp.concatenate([before, value, after], axis=dim)
    return value


def trimmed(array, axis, offset):
    index = [slice(None)] + [slice(1, -1)] * 3
    index[axis + 1] = slice(1 + offset, array.shape[axis + 1] - 1 + offset)
    return array[tuple(index)]


def advection(padded):
    total = None
    for axis in range(3):
        flux = padded[axis : axis + 1] * padded
        term = (trimmed(flux, axis, 1) - trimmed(flux, axis, -1)) * 0.5
        total = term if total is None else total + term
    return total


def apply_padded(padded, field, coefficient):
    beside = padded[:, 2:, 1:-1, 1:-1] + padded[:, :-2, 1:-1, 1:-1]
    beside = beside + padded[:, 1:-1, 2:, 1:-1] + padded[:, 1:-1, :-2, 1:-1]
    beside = beside + padded[:, 1:-1, 1:-1, 2:] + padded[:, 1:-1, 1:-1, :-2]
    return (1.0 + 6.0 * coefficient) * field - coefficient * beside


def operate(field, coefficient):
    padded = with_halo(field, (("gx", 1), ("gy", 2), ("gz", 3)), 1)
    return apply_padded(padded, field, coefficient)


def products(residual, image):
    sums = lax.psum(
        (jnp.sum(residual * residual, axis=(1, 2, 3)), jnp.sum(residual * image, axis=(1, 2, 3))),
        ("gx", "gy", "gz"),
    )
    return (sums[0][:, None, None, None], sums[1][:, None, None, None])


def valid_cells(block_index, block_total, count, margin):
    position = block_index * count - margin + jnp.arange(count + 2 * margin)
    return ((position >= 0) & (position < count * block_total)).astype(jnp.float32)


def inside_mask(velocity, margin):
    mask_x = valid_cells(lax.axis_index("gx"), lax.axis_size("gx"), velocity.shape[1], margin)
    mask_y = valid_cells(lax.axis_index("gy"), lax.axis_size("gy"), velocity.shape[2], margin)
    mask_z = valid_cells(lax.axis_index("gz"), lax.axis_size("gz"), velocity.shape[3], margin)
    return (mask_x[:, None, None] * mask_y[None, :, None] * mask_z[None, None, :])[None]


def identity_cut(field):
    return field


def body(velocity, diffusion):
    coefficient = diffusion[:, None, None, None]

    def apply_next(field):
        return operate(field, coefficient)

    cut = identity_cut
    margin = ITERS
    deep = with_halo(velocity, (("gx", 1), ("gy", 2), ("gz", 3)), margin + 1)
    inside = inside_mask(velocity, margin)
    section = (deep[:, 1:-1, 1:-1, 1:-1] - time_step * advection(deep)) * inside

    def apply_next(field):
        padded = jnp.pad(field, ((0, 0), (1, 1), (1, 1), (1, 1)))
        return apply_padded(padded, field, coefficient) * inside

    def cut(field):
        return field[:, margin:-margin, margin:-margin, margin:-margin]

    first_image = apply_next(section)
    solution = jnp.zeros_like(section)
    residual = section
    image = first_image
    norm_now, curvature = products(cut(residual), cut(image))
    step_size = norm_now / curvature
    direction = residual
    along = image
    for iteration in range(ITERS):
        solution = solution + step_size * direction
        residual = residual - step_size * along
        if iteration + 1 < ITERS:
            image = apply_next(residual)
            norm_next, curvature = products(cut(residual), cut(image))
            dir_ratio = norm_next / norm_now
            step_size = norm_next / (curvature - dir_ratio * norm_next / step_size)
            direction = residual + dir_ratio * direction
            along = image + dir_ratio * along
            norm_now = norm_next
    return (cut(solution), cut(residual))


def solution(mesh):
    return jax.shard_map(
        body,
        mesh=mesh,
        in_specs=(P(None, "gx", "gy", "gz"), P()),
        out_specs=(P(None, "gx", "gy", "gz"), P(None, "gx", "gy", "gz")),
        check_vma=False,
    )
```

profile of v0, /device:TPU:0, one launch (start us, length us, event | category | flops | bytes accessed | tf_op | source)
XLA Modules:
  0.0 171.6 jit_solution(14397215847008372498)
XLA Ops:
  0.6 1.0 fusion.37
  1.6 2.4 %collective-permute-start = (f32[3,4,16,128]{3,2,1,0:T(8,128)S(1)}, f32[3,4,16,128]{3,2,1,0:T(8,128)S(1)}, u32[]{:S(2)}, u32[]{:S(2)}) collective-permute-start(f32[3,4,16,128]{3,2,1,0:T(8,128)S(1)} %get-tuple-element.36), channel_id=1, source_target_pairs={{0,16},{1,17},{2,18},{3,19},{4,20},{5,21},{6,22},{7,23},{8,24},{9,... | collective-permute-start | bytes 294920 | tf_op jit(solution)/shard_map/ppermute | solution.py:19
  4.0 1.3 collective-permute-start.1
  5.4 0.9 constant_dynamic-update-slice_fusion.1
  6.4 0.8 collective-permute-done.1
  7.3 4.2 %collective-permute-start.2 = (f32[3,16,4,128]{3,1,2,0:T(8,128)S(1)}, f32[3,16,4,128]{3,1,2,0:T(8,128)S(1)}, u32[]{:S(2)}, u32[]{:S(2)}) collective-permute-start(f32[3,16,4,128]{3,1,2,0:T(8,128)S(1)} %copy.25), channel_id=1, source_target_pairs={{0,4},{4,8},{8,12},{1,5},{5,9},{9,13},{2,6},{6,10},{10,14},{3,7},{... | collective-permute-start | bytes 294920 | tf_op jit(solution)/shard_map/ppermute | solution.py:19
  11.5 1.3 collective-permute-start.3
  12.9 2.3 %copy.20 = f32[3,16,16,128]{2,1,3,0:T(8,128)} copy(f32[3,16,16,128]{3,2,1,0:T(8,128)S(1)} %constant_dynamic-update-slice_fusion) | data formatting | bytes 786432 | tf_op jit(solution)/shard_map/concatenate | solution.py:21
  15.2 2.3 %copy.19 = f32[3,16,4,128]{2,1,3,0:T(8,128)} copy(f32[3,16,4,128]{3,1,2,0:T(8,128)S(1)} %collective-permute-done.2) | data formatting | bytes 196608 | tf_op jit(solution)/shard_map/ppermute | solution.py:19
  17.5 0.7 collective-permute-done.3
  18.2 2.2 %copy.21 = f32[3,16,4,128]{2,1,3,0:T(8,128)} copy(f32[3,16,4,128]{3,1,2,0:T(8,128)S(1)} %collective-permute-done.3) | data formatting | bytes 196608 | tf_op jit(solution)/shard_map/ppermute | solution.py:20
  20.4 5.4 %pad_maximum_fusion = f32[3,16,24,128]{2,1,3,0:T(8,128)S(1)} fusion(f32[3,16,4,128]{2,1,3,0:T(8,128)} %copy.21, f32[3,16,16,128]{2,1,3,0:T(8,128)} %copy.20, f32[3,16,4,128]{2,1,3,0:T(8,128)} %copy.19), kind=kLoop, calls=%fused_computation | loop fusion | flops 294912 | bytes 1179648 | tf_op jit(solution)/shard_map/concatenate | solution.py:21
  25.8 0.7 fusion.35
  26.5 4.1 %collective-permute-start.4 = (f32[3,16,24,4]{2,1,3,0:T(8,128)}, f32[3,16,24,4]{2,1,3,0:T(8,128)}, u32[]{:S(2)}, u32[]{:S(2)}) collective-permute-start(f32[3,16,24,4]{2,1,3,0:T(8,128)} %get-tuple-element.21), channel_id=1, source_target_pairs={{0,1},{1,2},{2,3},{4,5},{5,6},{6,7},{8,9},{9,10},{10,11},{12,13},{... | collective-permute-start | bytes 55304 | tf_op jit(solution)/shard_map/ppermute | solution.py:19
  30.6 1.3 collective-permute-start.5
  31.9 1.8 %copy.23 = f32[3,16,24,128]{3,2,1,0:T(8,128)} copy(f32[3,16,24,128]{2,1,3,0:T(8,128)S(1)} %pad_maximum_fusion) | data formatting | bytes 1179648 | tf_op jit(solution)/shard_map/concatenate | solution.py:21
  33.8 1.3 copy.22
  35.1 2.4 %collective-permute-done.5 = f32[3,16,24,4]{2,1,3,0:T(8,128)} collective-permute-done((f32[3,16,24,4]{2,1,3,0:T(8,128)}, f32[3,16,24,4]{2,1,3,0:T(8,128)}, u32[]{:S(2)}, u32[]{:S(2)}) %collective-permute-start.5) | collective-permute-done | bytes 18464 | tf_op jit(solution)/shard_map/ppermute | solution.py:20
  37.4 1.2 copy.24
  38.7 0.5 pad_maximum_fusion.1
  39.3 0.3 broadcast_multiply_fusion.2
  39.6 1.7 fusion.27
  41.3 0.7 fusion.7
  42.3 40.3 %all-reduce.5 = (f32[3]{0:T(128)S(1)}, f32[3]{0:T(128)S(1)}) all-reduce(f32[3]{0:T(128)S(1)} %get-tuple-element.9, f32[3]{0:T(128)S(1)} %get-tuple-element.8), channel_id=1, replica_groups=mesh['gx'=2,'gy'=4,'gz'=4] {'gx','gy','gz'}, use_global_device_ids=true, to_apply=%region_1.2 | all-reduce | flops 6 | bytes 48 | tf_op jit(solution)/shard_map/psum | solution.py:53
  82.6 0.8 multiply_subtract_fusion.1
  83.3 0.7 fusion.15
  84.3 40.4 %all-reduce.4 = (f32[3]{0:T(128)S(1)}, f32[3]{0:T(128)S(1)}) all-reduce(f32[3]{0:T(128)S(1)} %get-tuple-element.7, f32[3]{0:T(128)S(1)} %get-tuple-element.6), channel_id=1, replica_groups=mesh['gx'=2,'gy'=4,'gz'=4] {'gx','gy','gz'}, use_global_device_ids=true, to_apply=%region_5.6 | all-reduce | flops 6 | bytes 48 | tf_op jit(solution)/shard_map/psum | solution.py:53
  124.8 2.8 %multiply_add_fusion = (f32[3,14,22,134]{3,2,1,0:T(8,128)}, f32[3,14,22,134]{3,2,1,0:T(8,128)S(1)}) fusion(f32[3]{0:T(128)S(1)} %get-tuple-element.20, f32[3,14,22,134]{3,2,1,0:T(8,128)S(1)} %multiply_subtract_fusion.1, f32[3]{0:T(128)S(1)} %get-tuple-element.18, f32[14,22,134]{2,1,0:T(8,128)S(1)} %broadcast_multiply_fusion.3, f32[3]{0:T(128)S(1)} %copy-done.2, ...), kind=kLoop, calls=%fused_computation.53 | loop fusion | flops 2723952 | bytes 2146192 | tf_op jit(solution)/shard_map/add | solution.py:112
  127.6 0.7 fusion.23
  128.3 1.0 copy-done.1
  129.6 39.6 %all-reduce.3 = (f32[3]{0:T(128)S(1)}, f32[3]{0:T(128)S(1)}) all-reduce(f32[3]{0:T(128)S(1)} %get-tuple-element.5, f32[3]{0:T(128)S(1)} %get-tuple-element.4), channel_id=1, replica_groups=mesh['gx'=2,'gy'=4,'gz'=4] {'gx','gy','gz'}, use_global_device_ids=true, to_apply=%region_9.10 | all-reduce | flops 6 | bytes 48 | tf_op jit(solution)/shard_map/psum | solution.py:53
  169.2 2.3 %fusion.31 = (f32[3,8,16,128]{3,2,1,0:T(8,128)}, f32[3,8,16,128]{3,2,1,0:T(8,128)}) fusion(f32[3,14,22,134]{3,2,1,0:T(8,128)} %get-tuple-element.23, f32[3,14,22,134]{3,2,1,0:T(8,128)} %copy-done.1, f32[3,14,22,134]{3,2,1,0:T(8,128)S(1)} %get-tuple-element.24, f32[3]{0:T(128)S(1)} %get-tuple-element.16, f32[3]{0:T(128)S(1)} %get-tuple-element.17, ...), kind=kLoop, calls=%fused_computation.64 | loop fusion | flops 638976 | bytes 1376316 | tf_op jit(solution)/shard_map/sub | solution.py:105
  (26 shorter events, 1.2 us)
Async XLA Ops:
  1.6 3.8 %collective-permute-start = (f32[3,4,16,128]{3,2,1,0:T(8,128)S(1)}, f32[3,4,16,128]{3,2,1,0:T(8,128)S(1)}, u32[]{:S(2)}, u32[]{:S(2)}) collective-permute-start(f32[3,4,16,128]{3,2,1,0:T(8,128)S(1)} %get-tuple-element.36), channel_id=1, source_target_pairs={{0,16},{1,17},{2,18},{3,19},{4,20},{5,21},{6,22},{7,23},{8,24},{9,... | collective-permute-start | bytes 294920 | tf_op jit(solution)/shard_map/ppermute | solution.py:19
  4.0 3.2 %collective-permute-start.1 = (f32[3,4,16,128]{3,2,1,0:T(8,128)S(1)}, f32[3,4,16,128]{3,2,1,0:T(8,128)S(1)}, u32[]{:S(2)}, u32[]{:S(2)}) collective-permute-start(f32[3,4,16,128]{3,2,1,0:T(8,128)S(1)} %get-tuple-element.35), channel_id=1, source_target_pairs={{16,0},{17,1},{18,2},{19,3},{20,4},{21,5},{22,6},{23,7},{24,8},{25... | collective-permute-start | bytes 294920 | tf_op jit(solution)/shard_map/ppermute | solution.py:20
  7.3 7.9 %collective-permute-start.2 = (f32[3,16,4,128]{3,1,2,0:T(8,128)S(1)}, f32[3,16,4,128]{3,1,2,0:T(8,128)S(1)}, u32[]{:S(2)}, u32[]{:S(2)}) collective-permute-start(f32[3,16,4,128]{3,1,2,0:T(8,128)S(1)} %copy.25), channel_id=1, source_target_pairs={{0,4},{4,8},{8,12},{1,5},{5,9},{9,13},{2,6},{6,10},{10,14},{3,7},{... | collective-permute-start | bytes 294920 | tf_op jit(solution)/shard_map/ppermute | solution.py:19
  11.5 6.7 %collective-permute-start.3 = (f32[3,16,4,128]{3,1,2,0:T(8,128)S(1)}, f32[3,16,4,128]{3,1,2,0:T(8,128)S(1)}, u32[]{:S(2)}, u32[]{:S(2)}) collective-permute-start(f32[3,16,4,128]{3,1,2,0:T(8,128)S(1)} %copy.26), channel_id=1, source_target_pairs={{4,0},{8,4},{12,8},{5,1},{9,5},{13,9},{6,2},{10,6},{14,10},{7,3},{... | collective-permute-start | bytes 294920 | tf_op jit(solution)/shard_map/ppermute | solution.py:20
  20.4 11.5 %copy-start.2 = (f32[3]{0:T(128)S(1)}, f32[3]{0:T(128)}, u32[]{:S(2)}) copy-start(f32[3]{0:T(128)} %param.3) | copy-start | bytes 40
  26.5 7.2 %collective-permute-start.4 = (f32[3,16,24,4]{2,1,3,0:T(8,128)}, f32[3,16,24,4]{2,1,3,0:T(8,128)}, u32[]{:S(2)}, u32[]{:S(2)}) collective-permute-start(f32[3,16,24,4]{2,1,3,0:T(8,128)} %get-tuple-element.21), channel_id=1, source_target_pairs={{0,1},{1,2},{2,3},{4,5},{5,6},{6,7},{8,9},{9,10},{10,11},{12,13},{... | collective-permute-start | bytes 55304 | tf_op jit(solution)/shard_map/ppermute | solution.py:19
  30.6 6.8 %collective-permute-start.5 = (f32[3,16,24,4]{2,1,3,0:T(8,128)}, f32[3,16,24,4]{2,1,3,0:T(8,128)}, u32[]{:S(2)}, u32[]{:S(2)}) collective-permute-start(f32[3,16,24,4]{2,1,3,0:T(8,128)} %get-tuple-element.22), channel_id=1, source_target_pairs={{1,0},{2,1},{3,2},{5,4},{6,5},{7,6},{9,8},{10,9},{11,10},{13,12},{... | collective-permute-start | bytes 55304 | tf_op jit(solution)/shard_map/ppermute | solution.py:20
  33.8 4.9 %copy-start = (f32[3,16,24,128]{3,2,1,0:T(8,128)S(1)}, f32[3,16,24,128]{3,2,1,0:T(8,128)}, u32[]{:S(2)}) copy-start(f32[3,16,24,128]{3,2,1,0:T(8,128)} %copy.23) | copy-start | bytes 1769476
  128.3 1.0 copy-start.1
where the time goes:
time: 172 us
  blocking collectives  120 us (70%)
  other arithmetic  17 us (10%)
  local copies, waits for them, and re-layouts  14.9 us (9%)
  starting transfers between devices  14.6 us (8%)
  waiting for transfers between devices  3.87 us (2%)
    psum x3, blocking collectives, products(): lax.psum((jnp.sum(residual * residual, axis=(1, 2, 3)), jnp.sum(residual...  120 us
    ppermute x3, starting transfers between devices, with_halo(): before = lax.ppermute(last, axis, up)  10.7 us
    concatenate x2, other arithmetic, with_halo(): value = jnp.concatenate([before, value, after], axis=dim)  5.97 us
    concatenate x3, local copies, waits for them, and re-layouts, with_halo(): value = jnp.concatenate([before, value, after], axis=dim)  4.11 us
    ppermute x3, starting transfers between devices, with_halo(): after = lax.ppermute(first, axis, down)  3.86 us
    ppermute x3, waiting for transfers between devices, with_halo(): after = lax.ppermute(first, axis, down)  3.86 us
    ppermute x2, local copies, waits for them, and re-layouts, with_halo(): before = lax.ppermute(last, axis, up)  3.58 us
    ppermute x2, local copies, waits for them, and re-layouts, with_halo(): after = lax.ppermute(first, axis, down)  3.45 us
  transfers between devices with their start and end apart: 6, of which 3 were waited for; matrix products, arithmetic and copies ran while one was open for 5% of the time, Pallas kernels for 0%

commit v1 on v0

v1 whole, which is shorter than its diff:
```python
import functools
import itertools

import jax
import jax.numpy as jnp
from jax import lax
from jax.experimental import pallas as pl
from jax.experimental.pallas import tpu as pltpu
from jax.sharding import PartitionSpec as P

AXES = ("gx", "gy", "gz")
MESH_IDS = pl.DeviceIdType.MESH
MARGIN = 4
PAIRS = ((0, 0), (0, 1), (1, 1), (0, 2), (1, 2), (2, 2), (2, 3))
time_step = 0.25
ONE_SHOT = 64


def around(sizes, moved):
    return tuple(lax.rem(lax.axis_index(a) + o, s) for a, o, s in zip(AXES, moved, sizes))


def groups_of(sizes):
    total = sizes[0] * sizes[1] * sizes[2]
    if total <= ONE_SHOT:
        return [(0, 1, 2)]
    return [(0,), (1,), (2,)]


def offsets_of(sizes, group):
    ranges = [range(sizes[k]) if k in group else range(1) for k in range(3)]
    return [o for o in itertools.product(*ranges) if any(o)]


def slot_of(sizes, group):
    slot = 0
    for k in group:
        slot = slot * sizes[k] + lax.axis_index(AXES[k])
    return slot


def kernel(sizes, diff_ref, v_ref, x_ref, r_ref, F, S0, S1, S2, S3, mask, SL, SH, RL, RH, pack, zlow, zhigh, Q, QR, row, *rest):
    groups = groups_of(sizes)
    gathered, (fs, fr, gs, gr) = rest[: len(groups)], rest[len(groups):]
    comps, X, Y, Z = v_ref.shape
    XR, YR, ZR = X + 2 * MARGIN, Y + 2 * MARGIN, 2 * Z
    tiles = Y // 8
    here = [lax.axis_index(a) for a in AXES]

    def exists(moved):
        ok = None
        for k in range(3):
            if moved[k]:
                place = here[k] + moved[k]
                one = (place >= 0) & (place < sizes[k])
                ok = one if ok is None else ok & one
        return ok

    peers = set()
    for group in groups:
        peers.update(offsets_of(sizes, group))
    for dx, dy in itertools.product((-1, 0, 1), (-1, 0, 1)):
        moved = (dx % sizes[0], dy % sizes[1], 0)
        if any(moved):
            peers.add(moved)
    peers = sorted(peers)
    barrier = pltpu.get_barrier_semaphore()

    for c in range(comps):
        F[c, X:XR, 0:Y, 0:Z] = jnp.zeros((XR - X, Y, Z), jnp.float32)
        F[c, X:XR, :, Z:ZR] = jnp.zeros((XR - X, YR, Z), jnp.float32)
    RL[...] = jnp.zeros_like(RL)
    RH[...] = jnp.zeros_like(RH)
    QR[...] = jnp.zeros_like(QR)
    zlow[...] = jnp.zeros_like(zlow)
    zhigh[...] = jnp.zeros_like(zhigh)
    for moved in peers:
        pl.semaphore_signal(barrier, inc=1, device_id=around(sizes, moved), device_id_type=MESH_IDS)

    lane = lax.broadcasted_iota(jnp.int32, (8, Z), 1)
    sub = lax.broadcasted_iota(jnp.int32, (8, Z), 0)
    for c in range(comps):
        packed = jnp.zeros((8, Z), jnp.float32)
        for x in range(X):
            for t in range(tiles):
                g = x * tiles + t
                rolled = pltpu.roll(v_ref[c, x, 8 * t : 8 * t + 8, :], (8 * g + MARGIN) % Z, 1)
                packed = jnp.where(lane // 8 == g, rolled, packed)
        pack[c] = packed
        SL[c] = v_ref[c, :, 0:MARGIN, :]
        SH[c] = v_ref[c, :, Y - MARGIN : Y, :]
    pl.semaphore_wait(barrier, len(peers))

    copies = []

    def send(src, dst, moved):
        k = len(copies)
        copy = pltpu.make_async_remote_copy(
            src_ref=src, dst_ref=dst, send_sem=fs.at[k], recv_sem=fr.at[k],
            device_id=tuple(h + m for h, m in zip(here, moved)), device_id_type=MESH_IDS,
        )
        copies.append((copy, moved))
        pl.when(exists(moved))(copy.start)

    def received(which):
        for copy, moved in which:
            pl.when(exists(tuple(-m for m in moved)))(copy.wait_recv)

    send(pack, zhigh, (0, 0, -1))
    send(pack, zlow, (0, 0, 1))
    z_copies = copies[:]
    send(SL, RH.at[:, 0:X], (0, -1, 0))
    send(SH, RL.at[:, 0:X], (0, 1, 0))
    D = MARGIN - 1
    for dx in (-1, 1):
        planes = pl.ds(0, D) if dx < 0 else pl.ds(X - D, D)
        landing = pl.ds(X, D) if dx < 0 else pl.ds(XR - D, D)
        send(SL.at[:, planes], RH.at[:, landing], (dx, -1, 0))
        send(SH.at[:, planes], RL.at[:, landing], (dx, 1, 0))
    send(v_ref.at[:, 0:MARGIN], F.at[:, X : X + MARGIN, 0:Y, 0:Z], (-1, 0, 0))
    send(v_ref.at[:, X - MARGIN : X], F.at[:, X + MARGIN : XR, 0:Y, 0:Z], (1, 0, 0))
    face_copies = copies[len(z_copies):]

    for c in range(comps):
        F[c, 0:X, 0:Y, 0:Z] = v_ref[c]
    yy = lax.broadcasted_iota(jnp.int32, (YR, ZR), 0)
    zz = lax.broadcasted_iota(jnp.int32, (YR, ZR), 1)
    yy = jnp.where(yy >= Y + MARGIN, yy - YR, yy) + here[1] * Y
    zz = jnp.where(zz >= Z + Z // 2, zz - ZR, zz) + here[2] * Z
    inside = (yy >= 0) & (yy < Y * sizes[1]) & (zz >= 0) & (zz < Z * sizes[2])
    mask[...] = jnp.where(inside, 1.0, 0.0).astype(jnp.float32)

    received(z_copies)
    for c in range(comps):
        Q[c] = jnp.where(lane % 8 < MARGIN, zlow[c], zhigh[c])
    steps = [m for m in itertools.product((-1, 0, 1), (-1, 0, 1)) if any(m)]
    for dx, dy in sorted(steps, key=lambda m: -abs(m[1])):
        send(Q, QR.at[(1 - dx) * 3 + (1 - dy)], (dx, dy, 0))
    q_copies = copies[len(z_copies) + len(face_copies):]
    own = 4
    for c in range(comps):
        for x in range(X):
            for t in range(tiles):
                g = x * tiles + t
                F[c, x, 8 * t : 8 * t + 8, Z:ZR] = pltpu.roll(Q[c], (Z - MARGIN - 8 * g) % Z, 1)

    received(face_copies)
    rows_of_y = [x for x in range(XR) if x < X + D or x >= XR - D]
    for c in range(comps):
        for x in rows_of_y:
            F[c, x, Y : Y + MARGIN, 0:Z] = RH[c, x]
            F[c, x, Y + MARGIN : YR, 0:Z] = RL[c, x]
        for x in (X + D, XR - D - 1):
            F[c, x, Y:YR, 0:Z] = jnp.zeros((YR - Y, Z), jnp.float32)
    received(q_copies)

    for c in range(comps):
        for x in rows_of_y:
            dx, at = (0, x) if x < X else ((1, x - X) if x < X + D else (-1, x - MARGIN - MARGIN))
            base = (dx + 1) * 3 + 1
            if dx:
                for t in range(tiles):
                    g = at * tiles + t
                    F[c, x, 8 * t : 8 * t + 8, Z:ZR] = pltpu.roll(QR[base, c], (Z - MARGIN - 8 * g) % Z, 1)
            above = pltpu.roll(QR[base + 1, c], (Z - MARGIN - 8 * (at * tiles)) % Z, 1)
            below = pltpu.roll(QR[base - 1, c], (Z - MARGIN - 8 * (at * tiles + tiles - 1)) % Z, 1)
            F[c, x, Y:YR, Z:ZR] = jnp.where(sub < MARGIN, above, below)

    def ring(i):
        return lax.rem(i, XR)

    def plane_mask(i):
        place = here[0] * X + i
        xin = (place >= XR) & (place < X * sizes[0] + XR)
        return mask[...] * jnp.where(xin, 1.0, 0.0).astype(jnp.float32)

    def section_plane(i, carry):
        at, after, before = ring(i), ring(i + 1), ring(i - 1)
        inner = plane_mask(i)
        v = [F[c, at] for c in range(comps)]
        va = [F[c, after] for c in range(comps)]
        vb = [F[c, before] for c in range(comps)]
        for c in range(comps):
            total = va[0] * va[c] - vb[0] * vb[c]
            fy = v[1] * v[c]
            total = total + (pltpu.roll(fy, YR - 1, 0) - pltpu.roll(fy, 1, 0))
            fz = v[2] * v[c]
            total = total + (pltpu.roll(fz, ZR - 1, 1) - pltpu.roll(fz, 1, 1))
            S0[c, at] = (v[c] - (0.5 * time_step) * total) * inner
        return carry

    lax.fori_loop(XR - D, XR + X + D, section_plane, 0)

    def beside(ref, c, i):
        f = ref[c, ring(i)]
        total = ref[c, ring(i + 1)] + ref[c, ring(i - 1)]
        total = total + (pltpu.roll(f, YR - 1, 0) + pltpu.roll(f, 1, 0))
        return total + (pltpu.roll(f, ZR - 1, 1) + pltpu.roll(f, 1, 1))

    def first_plane(i, carry):
        inner = plane_mask(i)
        for c in range(comps):
            S1[c, ring(i)] = beside(S0, c, i) * inner
        return carry

    lax.fori_loop(XR - 2, XR + X + 2, first_plane, 0)

    def second_plane(i, carry):
        inner = plane_mask(i)
        for c in range(comps):
            S2[c, ring(i)] = beside(S1, c, i) * inner - 6.0 * S0[c, ring(i)]
        return carry

    lax.fori_loop(XR - 1, XR + X + 1, second_plane, 0)

    def third_plane(i, sums):
        sums = list(sums)
        at = i - XR
        for c in range(comps):
            p = [S[c, at, 0:Y, 0:Z] for S in (S0, S1, S2)]
            p.append(beside(S2, c, i)[0:Y, 0:Z] - 9.0 * p[1])
            S3[c, at] = p[3]
            for k, (a, b) in enumerate(PAIRS):
                both = p[a] * p[b]
                part = both[0:8]
                for t in range(1, tiles):
                    part = part + both[8 * t : 8 * t + 8]
                sums[k * comps + c] = sums[k * comps + c] + part
        return tuple(sums)

    sums = lax.fori_loop(XR, XR + X, third_plane, (jnp.zeros((8, Z), jnp.float32),) * (comps * len(PAIRS)))
    line = jnp.zeros((8, Z), jnp.float32)
    for k, part in enumerate(sums):
        line = jnp.where(lane == k, jnp.sum(part, axis=1, keepdims=True), line)
    line = jnp.sum(line, axis=0, keepdims=True)

    order = 0
    for group, landing in zip(groups, gathered):
        mine = slot_of(sizes, group)
        row[...] = line
        landing[mine] = line
        offsets = offsets_of(sizes, group)
        for moved in offsets:
            pltpu.make_async_remote_copy(
                src_ref=row, dst_ref=landing.at[mine], send_sem=gs.at[order], recv_sem=gr.at[order],
                device_id=around(sizes, moved), device_id_type=MESH_IDS,
            ).start()
        many = landing.at[pl.ds(0, len(offsets))]
        pltpu.make_async_copy(many, many, gr.at[order]).wait()
        line = landing[0]
        for k in range(1, len(offsets) + 1):
            line = line + landing[k]
        pltpu.make_async_copy(many, many, gs.at[order]).wait()
        order += 1

    g = {}
    for k, (a, b) in enumerate(PAIRS):
        value = line if k == 0 else pltpu.roll(line, Z - k * comps, 1)
        g[a, b] = g[b, a] = value
    g[0, 3] = g[1, 2] - 9.0 * g[0, 1]
    g[1, 3] = g[2, 2] + 6.0 * g[0, 2] - 9.0 * g[1, 1]
    at_lane = lax.broadcasted_iota(jnp.int32, (1, Z), 1)
    coef = jnp.full((1, Z), 1.0, jnp.float32)
    for c in range(comps):
        coef = jnp.where(at_lane == c, diff_ref[c], coef)
    diagonal = 1.0 + 6.0 * coef
    zero = jnp.zeros((1, Z), jnp.float32)

    def image_of(d):
        return [
            diagonal * d[0] - 6.0 * coef * d[1],
            diagonal * d[1] - coef * (d[0] + 9.0 * d[2]),
            diagonal * d[2] - coef * d[1],
            -coef * d[2],
        ]

    def form(a, b):
        total = None
        for i, left in enumerate(a):
            for j, right in enumerate(b):
                if left is zero or right is zero:
                    continue
                term = left * right * g[i, j]
                total = term if total is None else total + term
        return total

    res = [zero + 1.0, zero, zero, zero]
    direction = [zero + 1.0, zero, zero]
    found = [zero, zero, zero]
    norm = g[0, 0]
    for iteration in range(3):
        image = image_of(direction)
        if iteration == 0:
            image = [image[0], image[1], zero, zero]
        elif iteration == 1:
            image = [image[0], image[1], image[2], zero]
        step = norm / form(direction, image)
        found = [f if d is zero else f + step * d for f, d in zip(found, direction)]
        res = [r if m is zero else r - step * m for r, m in zip(res, image)]
        if iteration < 2:
            after = form(res[:3], res[:3])
            ratio = after / norm
            direction = [r if d is zero else r + ratio * d for r, d in zip(res, direction)]
            norm = after

    for c in range(comps):
        def spread(value):
            return jnp.broadcast_to(jnp.sum(jnp.where(at_lane == c, value, 0.0), axis=1, keepdims=True), (Y, Z))

        fx = [spread(f) for f in found]
        fres = [spread(r) for r in res]
        for x in range(X):
            p = [S[c, x, 0:Y, 0:Z] for S in (S0, S1, S2)] + [S3[c, x]]
            x_ref[c, x] = fx[0] * p[0] + fx[1] * p[1] + fx[2] * p[2]
            r_ref[c, x] = fres[0] * p[0] + fres[1] * p[1] + fres[2] * p[2] + fres[3] * p[3]

    for copy, moved in copies:
        pl.when(exists(moved))(copy.wait_send)


def solution(mesh):
    sizes = tuple(mesh.shape[a] for a in AXES)
    groups = groups_of(sizes)

    def body(velocity, diffusion):
        comps, X, Y, Z = velocity.shape
        XR, YR, ZR = X + 2 * MARGIN, Y + 2 * MARGIN, 2 * Z
        f32 = jnp.float32
        whole = pltpu.VMEM((comps, XR, YR, ZR), f32)
        packed = pltpu.VMEM((comps, 8, Z), f32)
        counts = [len(offsets_of(sizes, group)) + 1 for group in groups]
        out = jax.ShapeDtypeStruct(velocity.shape, f32)
        return pl.pallas_call(
            functools.partial(kernel, sizes),
            out_shape=(out, out),
            in_specs=[pl.BlockSpec(memory_space=pltpu.SMEM), pl.BlockSpec(memory_space=pltpu.VMEM)],
            out_specs=(pl.BlockSpec(memory_space=pltpu.VMEM), pl.BlockSpec(memory_space=pltpu.VMEM)),
            scratch_shapes=[
                whole, whole, whole, whole,
                pltpu.VMEM((comps, X, Y, Z), f32),
                pltpu.VMEM((YR, ZR), f32),
                pltpu.VMEM((comps, X, MARGIN, Z), f32),
                pltpu.VMEM((comps, X, MARGIN, Z), f32),
                pltpu.VMEM((comps, XR, MARGIN, Z), f32),
                pltpu.VMEM((comps, XR, MARGIN, Z), f32),
                packed, packed, packed, packed,
                pltpu.VMEM((9, comps, 8, Z), f32),
                pltpu.VMEM((1, Z), f32),
                *[pltpu.VMEM((count, 1, Z), f32) for count in counts],
                pltpu.SemaphoreType.DMA((18,)),
                pltpu.SemaphoreType.DMA((18,)),
                pltpu.SemaphoreType.DMA((len(groups),)),
                pltpu.SemaphoreType.DMA((len(groups),)),
            ],
            compiler_params=pltpu.CompilerParams(collective_id=0, has_side_effects=True),
        )(diffusion, velocity)

    return jax.shard_map(
        body,
        mesh=mesh,
        in_specs=(P(None, "gx", "gy", "gz"), P()),
        out_specs=(P(None, "gx", "gy", "gz"), P(None, "gx", "gy", "gz")),
        check_vma=False,
    )
```

time: 172 us -> 26.3 us (0.15)
  blocking collectives: 120 us -> 0 us
  Pallas kernels: 0 us -> 23.2 us
  other arithmetic: 17 us -> 0 us
  starting transfers between devices: 14.6 us -> 0 us
  local copies, waits for them, and re-layouts: 14.9 us -> 2.34 us
  waiting for transfers between devices: 3.87 us -> 0 us
    psum x3 -> x0, blocking collectives: 120 us -> none  [products(): lax.psum((jnp.sum(residual * residual, axis=(1, 2, 3)), jnp.sum(residual...]
    pallas_call x0 -> x1, Pallas kernels: none -> 23.2 us  [body(): pl.pallas_call(functools.partial(kernel, sizes), out_shape=(out, out), in...]
    ppermute x6 -> x0, starting transfers between devices: 14.6 us -> none  [the longest x3 10.7 us: with_halo(): before = lax.ppermute(last, axis, up)]
    ppermute x4 -> x0, local copies, waits for them, and re-layouts: 7.03 us -> none  [the longest x2 3.58 us: with_halo(): before = lax.ppermute(last, axis, up)]
    concatenate x2 -> x0, other arithmetic: 5.97 us -> none  [with_halo(): value = jnp.concatenate([before, value, after], axis=dim)]
    mul x7 -> x0, other arithmetic: 4.29 us -> none  [the longest x3 2.11 us: apply_next(): return apply_padded(padded, field, coefficient) * inside]
    concatenate x3 -> x0, local copies, waits for them, and re-layouts: 4.11 us -> none  [with_halo(): value = jnp.concatenate([before, value, after], axis=dim)]
    ppermute x6 -> x0, waiting for transfers between devices: 3.87 us -> none  [the longest x3 3.86 us: with_halo(): after = lax.ppermute(first, axis, down)]
  transfers between devices with their start and end apart: 6 -> 0, of which waited for: 3 -> 0; matrix products, arithmetic and copies ran while one was open for 5% -> 0% of each run, Pallas kernels for 0% -> 0%
where the time goes in v1:
time: 26.3 us; the launch traced here: 26.2 us
  Pallas kernels  23.2 us (88%)
  local copies, waits for them, and re-layouts  2.34 us (9%)
  between operations  0.65 us (2%)
    pallas_call x1, Pallas kernels, body(): pl.pallas_call(functools.partial(kernel, sizes), out_shape=(out, out), in...  23.2 us
    unnamed x4, local copies, waits for them, and re-layouts  2.34 us

profile of v1, /device:TPU:0, one launch (start us, length us, event | category | flops | bytes accessed | tf_op | source)
XLA Modules:
  0.0 26.2 jit_solution(14691766984002814694)
XLA Ops:
  0.6 23.2 %shard_map.41 = (f32[3,8,16,128]{3,2,1,0:T(8,128)}, f32[3,8,16,128]{3,2,1,0:T(8,128)}) custom-call(f32[3]{0:T(128)} %diff_ref.1, f32[3,8,16,128]{3,2,1,0:T(8,128)} %v_ref.1), custom_call_target="tpu_custom_call" | custom-call | tf_op jit(solution)/shard_map/pallas_call | solution.py:333
  23.8 0.0 copy-start
  23.8 1.7 %copy.6 = f32[3,8,16,128]{3,2,1,0:T(8,128)} copy(f32[3,8,16,128]{3,2,1,0:T(8,128)} %get-tuple-element.4) | data formatting | bytes 393216
  25.5 0.0 copy-done
  25.5 0.7 %copy.7 = f32[3,8,16,128]{3,2,1,0:T(8,128)} copy(f32[3,8,16,128]{3,2,1,0:T(8,128)S(1)} %copy-done) | data formatting | bytes 393216
Async XLA Ops:
  23.8 1.7 %copy-start = (f32[3,8,16,128]{3,2,1,0:T(8,128)S(1)}, f32[3,8,16,128]{3,2,1,0:T(8,128)}, u32[]{:S(2)}) copy-start(f32[3,8,16,128]{3,2,1,0:T(8,128)} %get-tuple-element.5) | copy-start | bytes 589828

commit v2 on v1

--- a/solution.py
+++ b/solution.py
@@ -14,6 +14,7 @@
 PAIRS = ((0, 0), (0, 1), (1, 1), (0, 2), (1, 2), (2, 2), (2, 3))
 time_step = 0.25
 ONE_SHOT = 64
+GRANT = 16 * 1024 * 1024
 
 
 def around(sizes, moved):
@@ -39,10 +40,10 @@
     return slot
 
 
-def kernel(sizes, diff_ref, v_ref, x_ref, r_ref, F, S0, S1, S2, S3, mask, SL, SH, RL, RH, pack, zlow, zhigh, Q, QR, row, *rest):
+def kernel(sizes, diff_hbm, v_hbm, x_ref, r_ref, diff_ref, F, S0, S1, S2, S3, mask, SL, SH, RL, RH, pack, zlow, zhigh, Q, QR, row, *rest):
     groups = groups_of(sizes)
-    gathered, (fs, fr, gs, gr) = rest[: len(groups)], rest[len(groups):]
-    comps, X, Y, Z = v_ref.shape
+    gathered, (fs, fr, gs, gr, ins) = rest[: len(groups)], rest[len(groups):]
+    comps, X, Y, Z = v_hbm.shape
     XR, YR, ZR = X + 2 * MARGIN, Y + 2 * MARGIN, 2 * Z
     tiles = Y // 8
     here = [lax.axis_index(a) for a in AXES]
@@ -63,19 +64,58 @@
         moved = (dx % sizes[0], dy % sizes[1], 0)
         if any(moved):
             peers.add(moved)
-    peers = sorted(peers)
+    peers = sorted(peers, key=lambda o: -sum(min(m, s - m) for m, s in zip(o, sizes)))
     barrier = pltpu.get_barrier_semaphore()
 
-    for c in range(comps):
-        F[c, X:XR, 0:Y, 0:Z] = jnp.zeros((XR - X, Y, Z), jnp.float32)
-        F[c, X:XR, :, Z:ZR] = jnp.zeros((XR - X, YR, Z), jnp.float32)
-    RL[...] = jnp.zeros_like(RL)
-    RH[...] = jnp.zeros_like(RH)
-    QR[...] = jnp.zeros_like(QR)
-    zlow[...] = jnp.zeros_like(zlow)
-    zhigh[...] = jnp.zeros_like(zhigh)
     for moved in peers:
         pl.semaphore_signal(barrier, inc=1, device_id=around(sizes, moved), device_id_type=MESH_IDS)
+    own_cells = pltpu.make_async_copy(v_hbm, F.at[:, 0:X, 0:Y, 0:Z], ins.at[0])
+    own_cells.start()
+    own_diff = pltpu.make_async_copy(diff_hbm, diff_ref, ins.at[1])
+    own_diff.start()
+
+    def missing(moved):
+        return pl.when(jnp.logical_not(exists(moved)))
+
+    for c in range(comps):
+        F[c, X:XR, :, Z:ZR] = jnp.zeros((XR - X, YR, Z), jnp.float32)
+
+    @missing((1, 0, 0))
+    def _():
+        for c in range(comps):
+            F[c, X : X + MARGIN, 0:Y, 0:Z] = jnp.zeros((MARGIN, Y, Z), jnp.float32)
+
+    @missing((-1, 0, 0))
+    def _():
+        for c in range(comps):
+            F[c, X + MARGIN : XR, 0:Y, 0:Z] = jnp.zeros((MARGIN, Y, Z), jnp.float32)
+
+    D = MARGIN - 1
+    for dy, ref in ((-1, RL), (1, RH)):
+        for dx, first, count in ((0, 0, X), (1, X, D), (-1, XR - D, D)):
+            @missing((dx, dy, 0))
+            def _(ref=ref, first=first, count=count):
+                for c in range(comps):
+                    ref[c, first : first + count] = jnp.zeros((count, MARGIN, Z), jnp.float32)
+
+    for dx, dy in itertools.product((-1, 0, 1), (-1, 0, 1)):
+        if dx or dy:
+            @missing((dx, dy, 0))
+            def _(at=(dx + 1) * 3 + dy + 1):
+                QR[at] = jnp.zeros((comps, 8, Z), jnp.float32)
+
+    for dz, ref in ((-1, zlow), (1, zhigh)):
+        @missing((0, 0, dz))
+        def _(ref=ref):
+            ref[...] = jnp.zeros((comps, 8, Z), jnp.float32)
+
+    yy = lax.broadcasted_iota(jnp.int32, (YR, ZR), 0)
+    zz = lax.broadcasted_iota(jnp.int32, (YR, ZR), 1)
+    yy = jnp.where(yy >= Y + MARGIN, yy - YR, yy) + here[1] * Y
+    zz = jnp.where(zz >= Z + Z // 2, zz - ZR, zz) + here[2] * Z
+    inside = (yy >= 0) & (yy < Y * sizes[1]) & (zz >= 0) & (zz < Z * sizes[2])
+    mask[...] = jnp.where(inside, 1.0, 0.0).astype(jnp.float32)
+    own_cells.wait()
 
     lane = lax.broadcasted_iota(jnp.int32, (8, Z), 1)
     sub = lax.broadcasted_iota(jnp.int32, (8, Z), 0)
@@ -84,11 +124,11 @@
         for x in range(X):
             for t in range(tiles):
                 g = x * tiles + t
-                rolled = pltpu.roll(v_ref[c, x, 8 * t : 8 * t + 8, :], (8 * g + MARGIN) % Z, 1)
+                rolled = pltpu.roll(F[c, x, 8 * t : 8 * t + 8, 0:Z], (8 * g + MARGIN) % Z, 1)
                 packed = jnp.where(lane // 8 == g, rolled, packed)
         pack[c] = packed
-        SL[c] = v_ref[c, :, 0:MARGIN, :]
-        SH[c] = v_ref[c, :, Y - MARGIN : Y, :]
+        SL[c] = F[c, 0:X, 0:MARGIN, 0:Z]
+        SH[c] = F[c, 0:X, Y - MARGIN : Y, 0:Z]
     pl.semaphore_wait(barrier, len(peers))
 
     copies = []
@@ -111,24 +151,14 @@
     z_copies = copies[:]
     send(SL, RH.at[:, 0:X], (0, -1, 0))
     send(SH, RL.at[:, 0:X], (0, 1, 0))
-    D = MARGIN - 1
     for dx in (-1, 1):
         planes = pl.ds(0, D) if dx < 0 else pl.ds(X - D, D)
         landing = pl.ds(X, D) if dx < 0 else pl.ds(XR - D, D)
         send(SL.at[:, planes], RH.at[:, landing], (dx, -1, 0))
         send(SH.at[:, planes], RL.at[:, landing], (dx, 1, 0))
-    send(v_ref.at[:, 0:MARGIN], F.at[:, X : X + MARGIN, 0:Y, 0:Z], (-1, 0, 0))
-    send(v_ref.at[:, X - MARGIN : X], F.at[:, X + MARGIN : XR, 0:Y, 0:Z], (1, 0, 0))
+    send(F.at[:, 0:MARGIN, 0:Y, 0:Z], F.at[:, X : X + MARGIN, 0:Y, 0:Z], (-1, 0, 0))
+    send(F.at[:, X - MARGIN : X, 0:Y, 0:Z], F.at[:, X + MARGIN : XR, 0:Y, 0:Z], (1, 0, 0))
     face_copies = copies[len(z_copies):]
-
-    for c in range(comps):
-        F[c, 0:X, 0:Y, 0:Z] = v_ref[c]
-    yy = lax.broadcasted_iota(jnp.int32, (YR, ZR), 0)
-    zz = lax.broadcasted_iota(jnp.int32, (YR, ZR), 1)
-    yy = jnp.where(yy >= Y + MARGIN, yy - YR, yy) + here[1] * Y
-    zz = jnp.where(zz >= Z + Z // 2, zz - ZR, zz) + here[2] * Z
-    inside = (yy >= 0) & (yy < Y * sizes[1]) & (zz >= 0) & (zz < Z * sizes[2])
-    mask[...] = jnp.where(inside, 1.0, 0.0).astype(jnp.float32)
 
     received(z_copies)
     for c in range(comps):
@@ -189,7 +219,7 @@
             S0[c, at] = (v[c] - (0.5 * time_step) * total) * inner
         return carry
 
-    lax.fori_loop(XR - D, XR + X + D, section_plane, 0)
+    lax.fori_loop(XR - D, XR + X + D, section_plane, 0, unroll=True)
 
     def beside(ref, c, i):
         f = ref[c, ring(i)]
@@ -203,7 +233,7 @@
             S1[c, ring(i)] = beside(S0, c, i) * inner
         return carry
 
-    lax.fori_loop(XR - 2, XR + X + 2, first_plane, 0)
+    lax.fori_loop(XR - 2, XR + X + 2, first_plane, 0, unroll=True)
 
     def second_plane(i, carry):
         inner = plane_mask(i)
@@ -211,7 +241,7 @@
             S2[c, ring(i)] = beside(S1, c, i) * inner - 6.0 * S0[c, ring(i)]
         return carry
 
-    lax.fori_loop(XR - 1, XR + X + 1, second_plane, 0)
+    lax.fori_loop(XR - 1, XR + X + 1, second_plane, 0, unroll=True)
 
     def third_plane(i, sums):
         sums = list(sums)
@@ -228,7 +258,7 @@
                 sums[k * comps + c] = sums[k * comps + c] + part
         return tuple(sums)
 
-    sums = lax.fori_loop(XR, XR + X, third_plane, (jnp.zeros((8, Z), jnp.float32),) * (comps * len(PAIRS)))
+    sums = lax.fori_loop(XR, XR + X, third_plane, (jnp.zeros((8, Z), jnp.float32),) * (comps * len(PAIRS)), unroll=True)
     line = jnp.zeros((8, Z), jnp.float32)
     for k, part in enumerate(sums):
         line = jnp.where(lane == k, jnp.sum(part, axis=1, keepdims=True), line)
@@ -239,7 +269,7 @@
         mine = slot_of(sizes, group)
         row[...] = line
         landing[mine] = line
-        offsets = offsets_of(sizes, group)
+        offsets = [o for o in peers if o in offsets_of(sizes, group)]
         for moved in offsets:
             pltpu.make_async_remote_copy(
                 src_ref=row, dst_ref=landing.at[mine], send_sem=gs.at[order], recv_sem=gr.at[order],
@@ -260,6 +290,7 @@
     g[0, 3] = g[1, 2] - 9.0 * g[0, 1]
     g[1, 3] = g[2, 2] + 6.0 * g[0, 2] - 9.0 * g[1, 1]
     at_lane = lax.broadcasted_iota(jnp.int32, (1, Z), 1)
+    own_diff.wait()
     coef = jnp.full((1, Z), 1.0, jnp.float32)
     for c in range(comps):
         coef = jnp.where(at_lane == c, diff_ref[c], coef)
@@ -333,9 +364,10 @@
         return pl.pallas_call(
             functools.partial(kernel, sizes),
             out_shape=(out, out),
-            in_specs=[pl.BlockSpec(memory_space=pltpu.SMEM), pl.BlockSpec(memory_space=pltpu.VMEM)],
+            in_specs=[pl.BlockSpec(memory_space=pltpu.HBM)] * 2,
             out_specs=(pl.BlockSpec(memory_space=pltpu.VMEM), pl.BlockSpec(memory_space=pltpu.VMEM)),
             scratch_shapes=[
+                pltpu.SMEM((comps,), f32),
                 whole, whole, whole, whole,
                 pltpu.VMEM((comps, X, Y, Z), f32),
                 pltpu.VMEM((YR, ZR), f32),
@@ -351,8 +383,9 @@
                 pltpu.SemaphoreType.DMA((18,)),
                 pltpu.SemaphoreType.DMA((len(groups),)),
                 pltpu.SemaphoreType.DMA((len(groups),)),
+                pltpu.SemaphoreType.DMA((2,)),
             ],
-            compiler_params=pltpu.CompilerParams(collective_id=0, has_side_effects=True),
+            compiler_params=pltpu.CompilerParams(collective_id=0, has_side_effects=True, vmem_limit_bytes=GRANT),
         )(diffusion, velocity)
 
     return jax.shard_map(

time: 26.3 us -> 22.1 us (0.84)
  Pallas kernels: 23.2 us -> 18.3 us
  local copies, waits for them, and re-layouts: 2.34 us -> 2.93 us
    pallas_call x1, Pallas kernels: 23.2 us -> 18.3 us  [body(): pl.pallas_call(functools.partial(kernel, sizes), out_shape=(out, out), in...]
    unnamed x4 -> x6, local copies, waits for them, and re-layouts: 2.34 us -> 2.93 us
where the time goes in v2:
time: 22.1 us; the launch traced here: 21.9 us
  Pallas kernels  18.3 us (83%)
  local copies, waits for them, and re-layouts  2.93 us (13%)
  between operations  0.65 us (3%)
    pallas_call x1, Pallas kernels, body(): pl.pallas_call(functools.partial(kernel, sizes), out_shape=(out, out), in...  18.3 us
    unnamed x6, local copies, waits for them, and re-layouts  2.93 us

profile of v2, /device:TPU:0, one launch (start us, length us, event | category | flops | bytes accessed | tf_op | source)
XLA Modules:
  0.0 21.9 jit_solution(3483828869502330012)
XLA Ops:
  0.6 0.0 copy-start
  0.6 0.9 %copy-done = f32[3,8,16,128]{3,2,1,0:T(8,128)S(1)} copy-done((f32[3,8,16,128]{3,2,1,0:T(8,128)S(1)}, f32[3,8,16,128]{3,2,1,0:T(8,128)}, u32[]{:S(2)}) %copy-start) | copy-done | bytes 196632
  1.6 0.0 copy-start.1
  1.6 0.7 %copy-done.1 = f32[3]{0:T(128)S(1)} copy-done((f32[3]{0:T(128)S(1)}, f32[3]{0:T(128)}, u32[]{:S(2)}) %copy-start.1) | copy-done | bytes 36
  2.2 18.3 %shard_map.41 = (f32[3,8,16,128]{3,2,1,0:T(8,128)S(1)}, f32[3,8,16,128]{3,2,1,0:T(8,128)S(1)}) custom-call(f32[3]{0:T(128)S(1)} %copy-done.1, f32[3,8,16,128]{3,2,1,0:T(8,128)S(1)} %copy-done), custom_call_target="tpu_custom_call" | custom-call | tf_op jit(solution)/shard_map/pallas_call | solution.py:364
  20.6 0.7 %copy.6 = f32[3,8,16,128]{3,2,1,0:T(8,128)} copy(f32[3,8,16,128]{3,2,1,0:T(8,128)S(1)} %get-tuple-element.4) | data formatting | bytes 393216
  21.2 0.7 %copy.7 = f32[3,8,16,128]{3,2,1,0:T(8,128)} copy(f32[3,8,16,128]{3,2,1,0:T(8,128)S(1)} %get-tuple-element.5) | data formatting | bytes 393216
Async XLA Ops:
  0.6 0.9 %copy-start = (f32[3,8,16,128]{3,2,1,0:T(8,128)S(1)}, f32[3,8,16,128]{3,2,1,0:T(8,128)}, u32[]{:S(2)}) copy-start(f32[3,8,16,128]{3,2,1,0:T(8,128)} %v_hbm.1) | copy-start | bytes 589828
  1.6 0.7 %copy-start.1 = (f32[3]{0:T(128)S(1)}, f32[3]{0:T(128)}, u32[]{:S(2)}) copy-start(f32[3]{0:T(128)} %diff_hbm.1) | copy-start | bytes 40

commit v3 on v2

--- a/solution.py
+++ b/solution.py
@@ -14,7 +14,7 @@
 PAIRS = ((0, 0), (0, 1), (1, 1), (0, 2), (1, 2), (2, 2), (2, 3))
 time_step = 0.25
 ONE_SHOT = 64
-GRANT = 16 * 1024 * 1024
+GRANT = 66000000
 
 
 def around(sizes, moved):
@@ -42,7 +42,7 @@
 
 def kernel(sizes, diff_hbm, v_hbm, x_ref, r_ref, diff_ref, F, S0, S1, S2, S3, mask, SL, SH, RL, RH, pack, zlow, zhigh, Q, QR, row, *rest):
     groups = groups_of(sizes)
-    gathered, (fs, fr, gs, gr, ins) = rest[: len(groups)], rest[len(groups):]
+    gathered, (fs, fr, gs, gr, ins, waves) = rest[: len(groups)], rest[len(groups):]
     comps, X, Y, Z = v_hbm.shape
     XR, YR, ZR = X + 2 * MARGIN, Y + 2 * MARGIN, 2 * Z
     tiles = Y // 8
@@ -66,14 +66,41 @@
             peers.add(moved)
     peers = sorted(peers, key=lambda o: -sum(min(m, s - m) for m, s in zip(o, sizes)))
     barrier = pltpu.get_barrier_semaphore()
-
-    for moved in peers:
-        pl.semaphore_signal(barrier, inc=1, device_id=around(sizes, moved), device_id_type=MESH_IDS)
+    relayed = len(groups) == 1
+    greeted = [o for o in peers if not (relayed and o[2])]
+    beyond = ((0, 0, -1), (0, 0, 1)) if relayed else ()
+
+    def shifted(moved):
+        return tuple(h + m for h, m in zip(here, moved))
+
     own_cells = pltpu.make_async_copy(v_hbm, F.at[:, 0:X, 0:Y, 0:Z], ins.at[0])
     own_cells.start()
     own_diff = pltpu.make_async_copy(diff_hbm, diff_ref, ins.at[1])
     own_diff.start()
 
+    expected = len(greeted)
+    for moved in greeted:
+        pl.semaphore_signal(barrier, inc=1, device_id=around(sizes, moved), device_id_type=MESH_IDS)
+    for moved in beyond:
+        @pl.when(exists(moved))
+        def _(moved=moved):
+            pl.semaphore_signal(barrier, inc=1, device_id=shifted(moved), device_id_type=MESH_IDS)
+
+        expected = expected + exists(moved).astype(jnp.int32)
+
+    def announce(wave):
+        for k, moved in enumerate(beyond):
+            @pl.when(exists(moved))
+            def _(k=k, moved=moved):
+                pl.semaphore_signal(waves.at[wave, k], inc=1, device_id=shifted(moved), device_id_type=MESH_IDS)
+
+    def heard(wave):
+        for k, moved in enumerate(beyond):
+            @pl.when(exists(tuple(-m for m in moved)))
+            def _(k=k):
+                pl.semaphore_wait(waves.at[wave, k], 1)
+
+    last_wave = sizes[2] - 1
     def missing(moved):
         return pl.when(jnp.logical_not(exists(moved)))
 
@@ -129,7 +156,7 @@
         pack[c] = packed
         SL[c] = F[c, 0:X, 0:MARGIN, 0:Z]
         SH[c] = F[c, 0:X, Y - MARGIN : Y, 0:Z]
-    pl.semaphore_wait(barrier, len(peers))
+    pl.semaphore_wait(barrier, expected)
 
     copies = []
 
@@ -161,6 +188,8 @@
     face_copies = copies[len(z_copies):]
 
     received(z_copies)
+    if last_wave >= 2:
+        announce(2)
     for c in range(comps):
         Q[c] = jnp.where(lane % 8 < MARGIN, zlow[c], zhigh[c])
     steps = [m for m in itertools.product((-1, 0, 1), (-1, 0, 1)) if any(m)]
@@ -175,6 +204,10 @@
                 F[c, x, 8 * t : 8 * t + 8, Z:ZR] = pltpu.roll(Q[c], (Z - MARGIN - 8 * g) % Z, 1)
 
     received(face_copies)
+    if last_wave >= 2:
+        heard(2)
+    if last_wave >= 3:
+        announce(3)
     rows_of_y = [x for x in range(XR) if x < X + D or x >= XR - D]
     for c in range(comps):
         for x in rows_of_y:
@@ -264,6 +297,10 @@
         line = jnp.where(lane == k, jnp.sum(part, axis=1, keepdims=True), line)
     line = jnp.sum(line, axis=0, keepdims=True)
 
+    for wave in range(3, last_wave + 1):
+        heard(wave)
+        if wave < last_wave:
+            announce(wave + 1)
     order = 0
     for group, landing in zip(groups, gathered):
         mine = slot_of(sizes, group)
@@ -360,7 +397,7 @@
         whole = pltpu.VMEM((comps, XR, YR, ZR), f32)
         packed = pltpu.VMEM((comps, 8, Z), f32)
         counts = [len(offsets_of(sizes, group)) + 1 for group in groups]
-        out = jax.ShapeDtypeStruct(velocity.shape, f32)
+        out = pltpu.VMEM(velocity.shape, f32)
         return pl.pallas_call(
             functools.partial(kernel, sizes),
             out_shape=(out, out),
@@ -384,6 +421,7 @@
                 pltpu.SemaphoreType.DMA((len(groups),)),
                 pltpu.SemaphoreType.DMA((len(groups),)),
                 pltpu.SemaphoreType.DMA((2,)),
+                pltpu.SemaphoreType.REGULAR((sizes[2], 2)),
             ],
             compiler_params=pltpu.CompilerParams(collective_id=0, has_side_effects=True, vmem_limit_bytes=GRANT),
         )(diffusion, velocity)

time: 22.1 us -> 20.3 us (0.919)
  local copies, waits for them, and re-layouts: 2.93 us -> 1.36 us
    unnamed x6 -> x2, local copies, waits for them, and re-layouts: 2.93 us -> 1.36 us
where the time goes in v3:
time: 20.3 us; the launch traced here: 20.2 us
  Pallas kernels  18.2 us (90%)
  local copies, waits for them, and re-layouts  1.36 us (7%)
  between operations  0.64 us (3%)
    pallas_call x1, Pallas kernels, body(): pl.pallas_call(functools.partial(kernel, sizes), out_shape=(out, out), in...  18.2 us
    unnamed x2, local copies, waits for them, and re-layouts  1.36 us

profile of v3, /device:TPU:0, one launch (start us, length us, event | category | flops | bytes accessed | tf_op | source)
XLA Modules:
  0.0 20.2 jit_solution(10628829051989994744)
XLA Ops:
  0.6 18.2 %shard_map.41 = (f32[3,8,16,128]{3,2,1,0:T(8,128)S(1)}, f32[3,8,16,128]{3,2,1,0:T(8,128)S(1)}) custom-call(f32[3]{0:T(128)} %diff_hbm.1, f32[3,8,16,128]{3,2,1,0:T(8,128)} %v_hbm.1), custom_call_target="tpu_custom_call" | custom-call | tf_op jit(solution)/shard_map/pallas_call | solution.py:401
  18.8 0.7 %copy.6 = f32[3,8,16,128]{3,2,1,0:T(8,128)} copy(f32[3,8,16,128]{3,2,1,0:T(8,128)S(1)} %get-tuple-element.2) | data formatting | bytes 393216
  19.5 0.7 %copy.7 = f32[3,8,16,128]{3,2,1,0:T(8,128)} copy(f32[3,8,16,128]{3,2,1,0:T(8,128)S(1)} %get-tuple-element.3) | data formatting | bytes 393216

commit v4 on v3

--- a/solution.py
+++ b/solution.py
@@ -154,8 +154,6 @@
                 rolled = pltpu.roll(F[c, x, 8 * t : 8 * t + 8, 0:Z], (8 * g + MARGIN) % Z, 1)
                 packed = jnp.where(lane // 8 == g, rolled, packed)
         pack[c] = packed
-        SL[c] = F[c, 0:X, 0:MARGIN, 0:Z]
-        SH[c] = F[c, 0:X, Y - MARGIN : Y, 0:Z]
     pl.semaphore_wait(barrier, expected)
 
     copies = []
@@ -176,27 +174,30 @@
     send(pack, zhigh, (0, 0, -1))
     send(pack, zlow, (0, 0, 1))
     z_copies = copies[:]
+    for c in range(comps):
+        SL[c] = F[c, 0:X, 0:MARGIN, 0:Z]
+        SH[c] = F[c, 0:X, Y - MARGIN : Y, 0:Z]
     send(SL, RH.at[:, 0:X], (0, -1, 0))
     send(SH, RL.at[:, 0:X], (0, 1, 0))
+    send(F.at[:, 0:MARGIN, 0:Y, 0:Z], F.at[:, X : X + MARGIN, 0:Y, 0:Z], (-1, 0, 0))
+    send(F.at[:, X - MARGIN : X, 0:Y, 0:Z], F.at[:, X + MARGIN : XR, 0:Y, 0:Z], (1, 0, 0))
+    face_copies = copies[len(z_copies):]
+
+    received(z_copies)
+    if last_wave >= 2:
+        announce(2)
+    for c in range(comps):
+        Q[c] = jnp.where(lane % 8 < MARGIN, zlow[c], zhigh[c])
+    steps = [m for m in itertools.product((-1, 0, 1), (-1, 0, 1)) if any(m)]
+    for dx, dy in sorted(steps, key=lambda m: -abs(m[1])):
+        send(Q, QR.at[(1 - dx) * 3 + (1 - dy)], (dx, dy, 0))
+    q_copies = copies[len(z_copies) + len(face_copies):]
     for dx in (-1, 1):
         planes = pl.ds(0, D) if dx < 0 else pl.ds(X - D, D)
         landing = pl.ds(X, D) if dx < 0 else pl.ds(XR - D, D)
         send(SL.at[:, planes], RH.at[:, landing], (dx, -1, 0))
         send(SH.at[:, planes], RL.at[:, landing], (dx, 1, 0))
-    send(F.at[:, 0:MARGIN, 0:Y, 0:Z], F.at[:, X : X + MARGIN, 0:Y, 0:Z], (-1, 0, 0))
-    send(F.at[:, X - MARGIN : X, 0:Y, 0:Z], F.at[:, X + MARGIN : XR, 0:Y, 0:Z], (1, 0, 0))
-    face_copies = copies[len(z_copies):]
-
-    received(z_copies)
-    if last_wave >= 2:
-        announce(2)
-    for c in range(comps):
-        Q[c] = jnp.where(lane % 8 < MARGIN, zlow[c], zhigh[c])
-    steps = [m for m in itertools.product((-1, 0, 1), (-1, 0, 1)) if any(m)]
-    for dx, dy in sorted(steps, key=lambda m: -abs(m[1])):
-        send(Q, QR.at[(1 - dx) * 3 + (1 - dy)], (dx, dy, 0))
-    q_copies = copies[len(z_copies) + len(face_copies):]
-    own = 4
+    late_copies = copies[len(z_copies) + len(face_copies) + len(q_copies) :]
     for c in range(comps):
         for x in range(X):
             for t in range(tiles):
@@ -204,6 +205,7 @@
                 F[c, x, 8 * t : 8 * t + 8, Z:ZR] = pltpu.roll(Q[c], (Z - MARGIN - 8 * g) % Z, 1)
 
     received(face_copies)
+    received(late_copies)
     if last_wave >= 2:
         heard(2)
     if last_wave >= 3:

time: 20.3 us -> 19.9 us (0.980)
  Pallas kernels: 18.2 us -> 17.8 us
    pallas_call x1, Pallas kernels: 18.2 us -> 17.8 us  [body(): pl.pallas_call(functools.partial(kernel, sizes), out_shape=(out, out), in...]
where the time goes in v4:
time: 19.9 us; the launch traced here: 19.8 us
  Pallas kernels  17.8 us (89%)
  local copies, waits for them, and re-layouts  1.36 us (7%)
  between operations  0.64 us (3%)
    pallas_call x1, Pallas kernels, body(): pl.pallas_call(functools.partial(kernel, sizes), out_shape=(out, out), in...  17.8 us
    unnamed x2, local copies, waits for them, and re-layouts  1.36 us

profile of v4, /device:TPU:0, one launch (start us, length us, event | category | flops | bytes accessed | tf_op | source)
XLA Modules:
  0.0 19.8 jit_solution(1852149029068269705)
XLA Ops:
  0.6 17.8 %shard_map.41 = (f32[3,8,16,128]{3,2,1,0:T(8,128)S(1)}, f32[3,8,16,128]{3,2,1,0:T(8,128)S(1)}) custom-call(f32[3]{0:T(128)} %diff_hbm.1, f32[3,8,16,128]{3,2,1,0:T(8,128)} %v_hbm.1), custom_call_target="tpu_custom_call" | custom-call | tf_op jit(solution)/shard_map/pallas_call | solution.py:403
  18.4 0.7 %copy.6 = f32[3,8,16,128]{3,2,1,0:T(8,128)} copy(f32[3,8,16,128]{3,2,1,0:T(8,128)S(1)} %get-tuple-element.2) | data formatting | bytes 393216
  19.1 0.7 %copy.7 = f32[3,8,16,128]{3,2,1,0:T(8,128)} copy(f32[3,8,16,128]{3,2,1,0:T(8,128)S(1)} %get-tuple-element.3) | data formatting | bytes 393216
